TPU v7x, 256 devices: a whole 4x4x8 slice. The times are simulated.
256 devices in a mesh: grp: 8 (over x_lo, y), tile: 32 (over z, x_hi, core).
Axes of the slice: x: 4 (x_hi: 2, x_lo: 2; x = x_hi * 2 + x_lo), y: 4, z: 8, core: 2. Of those that a mesh axis runs over, the one named last changes fastest.
Arguments:
- latents: bfloat16 [8, 4096, 1152], P('grp', 'tile'), may hold values from -6 to 6
- condition: bfloat16 [8, 1152], replicated, may hold values from -6 to 6
- w_modulate: bfloat16 [1152, 3456], P(None, 'grp'), may hold values from -1 to 1
- w_project: bfloat16 [1152, 3456], replicated, may hold values from -0.1875 to 0.1875
- w_output: bfloat16 [1152, 1152], replicated, may hold values from -0.1875 to 0.1875
- detail: int32 [8, 32], P('grp'), may hold values from 0 to 1, as said below
Outputs:
- updated: bfloat16 [8, 4096, 1152], P('grp', 'tile')
Inputs may be any that keep to these rules, and one draw needn't show every extreme that they name: `detail`: at most 8 strips of an image are marked, and at least one.
All inputs are finite; a program needn't handle non-finite values.
Results may differ from a plain program's by a relative error of at most 0.012.
Values may be sent and summed in bfloat16 or wider, within the bound.
A program may use at most 192 MiB of HBM per device.

v0:
```python
import jax
import jax.numpy as jnp
from jax import lax
from jax.sharding import PartitionSpec as P

HEADS = 16
ROW_TOKENS = 64


def with_halo(cells, sides, width):
    for axis, dim in sides:
        count = lax.axis_size(axis)
        ends = count - 1
        head = lax.slice_in_dim(cells, 0, width, axis=dim)
        tail = lax.slice_in_dim(cells, cells.shape[dim] - width, cells.shape[dim], axis=dim)
        cells = jnp.concatenate(
            [
                lax.ppermute(tail, axis, [(i, (i + 1) % count) for i in range(ends)]),
                cells,
                lax.ppermute(head, axis, [((i + 1) % count, i) for i in range(ends)]),
            ],
            axis=dim,
        )
    return cells


def partial_attend(query, keys, values, valid):
    count = query.shape[0]
    width = query.shape[1]
    heads_q = query.reshape(count, HEADS, width // HEADS)
    heads_k = keys.reshape(keys.shape[0], HEADS, width // HEADS)
    heads_v = values.reshape(values.shape[0], HEADS, width // HEADS)
    scores = jnp.einsum("qhd,khd->hqk", heads_q, heads_k, preferred_element_type=jnp.float32)
    scores = scores / jnp.sqrt(jnp.float32(width // HEADS))
    if valid is not None:
        scores = jnp.where(valid[None, None, :], scores, jnp.float32(-1e30))
    top = jnp.max(scores, axis=2)
    probs = jnp.exp(scores - top[:, :, None])
    total = jnp.sum(probs, axis=2)
    result = jnp.einsum(
        "hqk,khd->qhd", probs.astype(jnp.bfloat16), heads_v, preferred_element_type=jnp.float32
    )
    return (result.reshape(count, width), top, total)


def finish(result, total):
    count = result.shape[0]
    heads = total.shape[0]
    return (result.reshape(count, heads, -1) / jnp.transpose(total)[:, :, None]).reshape(count, -1)


def blend(first, second):
    sum_first, top_first, total_first = first
    sum_second, top_second, total_second = second
    merged = jnp.maximum(top_first, top_second)
    old_factor = jnp.exp(top_first - merged)
    new_factor = jnp.exp(top_second - merged)
    rows = sum_first.shape[0]
    heads = top_first.shape[0]
    scaled = sum_first.reshape(rows, heads, -1) * jnp.transpose(old_factor)[:, :, None]
    scaled = sum_second.reshape(rows, heads, -1) * jnp.transpose(new_factor)[:, :, None]
    return (scaled.reshape(sum_first.shape), merged, total_second * new_factor)


def on_device(latents, condition, w_modulate, w_project, w_output, detail):
    width = w_output.shape[0]
    columns = jnp.dot(condition, w_modulate, preferred_element_type=jnp.float32)
    modulation = lax.all_to_all(columns, "grp", split_axis=0, concat_axis=1, tiled=True)
    shift = modulation[:, :width]
    scale = modulation[:, width : 2 * width]
    gate = modulation[:, 2 * width :]
    tokens = latents[0]
    count = tokens.shape[0]
    values32 = tokens.astype(jnp.float32)
    mean = jnp.mean(values32, axis=1, keepdims=True)
    centered = values32 - mean
    variance = jnp.mean(centered * centered, axis=1, keepdims=True)
    normed = (centered / jnp.sqrt(variance + 1e-06) * (1.0 + scale) + shift).astype(jnp.bfloat16)
    projected = jnp.dot(normed, w_project, preferred_element_type=jnp.float32).astype(jnp.bfloat16)
    query = projected[:, :width]
    pairs = projected[:, width:]
    extended = with_halo(pairs, (("tile", 0),), ROW_TOKENS)
    position = lax.axis_index("tile")
    strips = lax.axis_size("tile")
    valid = jnp.concatenate(
        [
            jnp.broadcast_to(position > 0, (ROW_TOKENS,)),
            jnp.ones((count,), dtype=bool),
            jnp.broadcast_to(position < strips - 1, (ROW_TOKENS,)),
        ]
    )
    near_sum, near_top, near_total = partial_attend(
        query, extended[:, :width], extended[:, width:], valid
    )
    near = finish(near_sum, near_total)
    marks = detail[0]
    mark = lax.dynamic_index_in_dim(marks, position, keepdims=False)
    start_state = (
        jnp.zeros((count, width), jnp.float32),
        jnp.full((HEADS, count), -1e30, jnp.float32),
        jnp.zeros((HEADS, count), jnp.float32),
    )
    piece = lax.all_gather(pairs, "tile", axis=0, tiled=True)

    def update(state):
        return blend(state, partial_attend(query, piece[:, :width], piece[:, width:], None))

    def keep_state(state):
        return state

    whole_sum, whole_top, whole_total = lax.cond(mark > 0, update, keep_state, start_state)
    whole = finish(whole_sum, jnp.where(whole_total > 0, whole_total, 1.0))
    mixed = (near + jnp.where(mark > 0, whole, 0.0)).astype(jnp.bfloat16)
    branch = jnp.dot(mixed, w_output, preferred_element_type=jnp.float32)
    updated = (values32 + gate * branch).astype(jnp.bfloat16)
    return updated[None]


def solution(mesh):
    in_specs = (P("grp", "tile", None), P(), P(None, "grp"), P(), P(), P("grp", None))
    out_specs = P("grp", "tile", None)
    return jax.shard_map(
        on_device, mesh=mesh, in_specs=in_specs, out_specs=out_specs, check_vma=False
    )
```

profile of v0, /device:TPU:99, one launch (start us, length us, event | category | flops | bytes accessed | tf_op | source)
XLA Modules:
  0.0 271.4 jit_solution(16157270342811202824)
XLA Ops:
  6.5 1.7 convolution_bitcast_fusion.1
  8.9 5.4 %all-to-all-start = ((f32[8,1,432]{2,1,0:T(1,128)}), f32[8,1,432]{2,1,0:T(1,128)S(1)}, u32[]{:S(2)}, u32[]{:S(2)}) async-start(f32[8,1,432]{2,1,0:T(1,128)} %copy.17), calls=%async_computation | async-start | bytes 32768 | tf_op jit(solution)/shard_map/all_to_all | solution.py:68
  15.4 1.2 fusion.31
  16.6 1.6 all-to-all-done
  18.4 4.8 %convolution_convert_fusion = bf16[128,3456]{1,0:T(8,128)(2,1)S(1)} fusion(bf16[1152,3456]{1,0:T(8,128)(2,1)} %param.11, bf16[1,128,1152]{2,1,0:T(8,128)(2,1)} %param.8, f32[1152]{0:T(1024)S(1)} %get-tuple-element.22, f32[1152]{0:T(1024)S(1)} %get-tuple-element.23, f32[128]{0:T(128)S(1)} %add_sqrt_fusion, f32[128]{0:T(128)S(1)} %broadcast_multiply_fusion), kind=kOutput, calls=%fused_computation.15 | convolution fusion | flops 1020542976 | bytes 9152512 | tf_op jit(solution)/shard_map/dot_general | solution.py:79
  25.1 2.0 fusion.49
  27.0 5.7 %collective-permute-start = (bf16[64,2304]{1,0:T(8,128)(2,1)}, bf16[64,2304]{1,0:T(8,128)(2,1)}, u32[]{:S(2)}, u32[]{:S(2)}) collective-permute-start(bf16[64,2304]{1,0:T(8,128)(2,1)} %get-tuple-element.30), channel_id=1, source_target_pairs={{0,1},{1,2},{2,3},{3,4},{4,5},{5,6},{6,7},{7,8},{8,9},{9,10},{10,1... | collective-permute-start | bytes 884744 | tf_op jit(solution)/shard_map/ppermute | solution.py:18
  32.8 1.9 collective-permute-start.1
  37.9 4.7 %collective-permute-done.1 = bf16[64,2304]{1,0:T(8,128)(2,1)} collective-permute-done((bf16[64,2304]{1,0:T(8,128)(2,1)}, bf16[64,2304]{1,0:T(8,128)(2,1)}, u32[]{:S(2)}, u32[]{:S(2)}) %collective-permute-start.1) | collective-permute-done | bytes 294944 | tf_op jit(solution)/shard_map/ppermute | solution.py:20
  42.6 1.1 pad_maximum_fusion
  43.7 1.1 fusion.48
  44.9 1.3 copy.20
  46.2 2.1 copy.18
  48.3 1.6 fusion.19
  50.9 1.5 fusion.22
  52.3 123.6 %all-gather.2.cloned.1.call-done = bf16[4096,2304]{1,0:T(8,128)(2,1)} async-done(((bf16[128,2304]{1,0:T(8,128)(2,1)}), bf16[4096,2304]{1,0:T(8,128)(2,1)}) %all-gather.2.cloned.1.call-update) | async-done | bytes 18874384 | tf_op jit(solution)/shard_map/all_gather | solution.py:103
  175.9 85.3 %conditional.1 = (f32[128,1152]{0,1:T(8,128)}, f32[16,128]{1,0:T(8,128)S(1)}) conditional(s32[]{:T(128)} %convert_element_type.32, () %tuple.13, (bf16[128,1152]{1,0:T(8,128)(2,1)S(1)}, bf16[4096,2304]{1,0:T(8,128)(2,1)}) %tuple.14), branch_computations={%region_4.5_spmd, %region_5.8_spmd} | conditional | flops 2483181568 | bytes 196591632 | solution.py:111
  175.9 23.7 %copy.22 = bf16[4096,2304]{0,1:T(8,128)(2,1)} copy(bf16[4096,2304]{1,0:T(8,128)(2,1)} %get-tuple-element.20) | data formatting | bytes 37748736 | tf_op jit(solution)/shard_map
  199.6 15.1 %fusion.47 = (bf16[4096,1152]{0,1:T(8,128)(2,1)}, bf16[4096,1152]{0,1:T(8,128)(2,1)}) fusion(bf16[4096,2304]{0,1:T(8,128)(2,1)} %copy.22), kind=kLoop, calls=%fused_computation.62 | loop fusion | bytes 37748736 | tf_op jit(solution)/shard_map/cond/branch_1_fun/slice | solution.py:106
  214.9 15.5 %multiply_reduce_fusion = (f32[16,128]{1,0:T(8,128)S(1)}, f32[16,128,4096]{2,1,0:T(8,128)}) fusion(bf16[128,16,72]{0,2,1:T(8,128)(2,1)S(1)} %bitcast.68, bf16[4096,16,72]{0,2,1:T(8,128)(2,1)} %bitcast.66), kind=kOutput, calls=%fused_computation.1 | convolution fusion | flops 1224734720 | bytes 43294720 | tf_op jit(solution)/shard_map/cond/branch_1_fun/qhd,khd->hqk/dot_general | solution.py:33
  230.3 16.9 %fusion.9 = f32[128,16,72]{0,2,1:T(8,128)} fusion(bf16[4096,16,72]{0,2,1:T(8,128)(2,1)} %bitcast.65, f32[16,128,4096]{2,1,0:T(8,128)} %get-tuple-element.27, f32[16,128]{1,0:T(8,128)S(1)} %get-tuple-element.26, f32[128,16]{0,1:T(8,128)S(1)} %fusion.12), kind=kOutput, calls=%fused_computation.8 | convolution fusion | flops 1233272832 | bytes 43597824 | tf_op jit(solution)/shard_map/cond/branch_1_fun/hqk,khd->qhd/dot_general | solution.py:40
  247.2 14.0 %fusion = f32[16,128]{1,0:T(8,128)S(1)} fusion(f32[16,128,4096]{2,1,0:T(8,128)} %get-tuple-element.27, f32[16,128]{1,0:T(8,128)S(1)} %get-tuple-element.26), kind=kLoop, calls=%fused_computation.2 | loop fusion | flops 25163776 | bytes 33570816 | tf_op jit(solution)/shard_map/cond/branch_1_fun/reduce_sum | solution.py:39
  261.3 2.0 fusion.37
  263.3 1.3 fusion.18
  (35 shorter events, 7.5 us)
Async XLA Ops:
  6.5 256.7 %copy-start = (bf16[1152,1152]{1,0:T(8,128)(2,1)S(1)}, bf16[1152,1152]{1,0:T(8,128)(2,1)}, u32[]{:S(2)}) copy-start(bf16[1152,1152]{1,0:T(8,128)(2,1)} %param.12) | copy-start | bytes 7962628
  8.9 9.3 %all-to-all-start = ((f32[8,1,432]{2,1,0:T(1,128)}), f32[8,1,432]{2,1,0:T(1,128)S(1)}, u32[]{:S(2)}, u32[]{:S(2)}) async-start(f32[8,1,432]{2,1,0:T(1,128)} %copy.17), calls=%async_computation | async-start | bytes 32768 | tf_op jit(solution)/shard_map/all_to_all | solution.py:68
  14.3 161.6 %all-gather.2.cloned.1.call-start = ((), (), s32[]{:S(2)}) async-start(), calls=%async_computation.1 | async-start | bytes 19464192 | tf_op jit(solution)/shard_map/all_gather | solution.py:103
  23.2 0.9 copy-start.3
  24.2 10.5 %copy-start.5 = (s32[1,32]{1,0:T(1,128)S(1)}, s32[1,32]{1,0:T(1,128)}, u32[]{:S(2)}) copy-start(s32[1,32]{1,0:T(1,128)} %param.13) | copy-start | bytes 388
  25.0 17.6 %copy-start.1 = (bf16[128,2304]{1,0:T(8,128)(2,1)S(1)}, bf16[128,2304]{1,0:T(8,128)(2,1)}, u32[]{:S(2)}) copy-start(bf16[128,2304]{1,0:T(8,128)(2,1)} %slice.50) | copy-start | bytes 1769476
  27.0 10.9 %collective-permute-start = (bf16[64,2304]{1,0:T(8,128)(2,1)}, bf16[64,2304]{1,0:T(8,128)(2,1)}, u32[]{:S(2)}, u32[]{:S(2)}) collective-permute-start(bf16[64,2304]{1,0:T(8,128)(2,1)} %get-tuple-element.30), channel_id=1, source_target_pairs={{0,1},{1,2},{2,3},{3,4},{4,5},{5,6},{6,7},{7,8},{8,9},{9,10},{10,1... | collective-permute-start | bytes 884744 | tf_op jit(solution)/shard_map/ppermute | solution.py:18
  32.8 9.9 %collective-permute-start.1 = (bf16[64,2304]{1,0:T(8,128)(2,1)}, bf16[64,2304]{1,0:T(8,128)(2,1)}, u32[]{:S(2)}, u32[]{:S(2)}) collective-permute-start(bf16[64,2304]{1,0:T(8,128)(2,1)} %get-tuple-element.31), channel_id=1, source_target_pairs={{1,0},{2,1},{3,2},{4,3},{5,4},{6,5},{7,6},{8,7},{9,8},{10,9},{11,1... | collective-permute-start | bytes 884744 | tf_op jit(solution)/shard_map/ppermute | solution.py:20
  48.3 2.6 copy-start.4
  175.9 87.3 %copy-start.2 = (bf16[1,128,1152]{2,1,0:T(8,128)(2,1)S(1)}, bf16[1,128,1152]{2,1,0:T(8,128)(2,1)}, u32[]{:S(2)}) copy-start(bf16[1,128,1152]{2,1,0:T(8,128)(2,1)} %param.8) | copy-start | bytes 884740
Sparse Core Ops, SparseCore 0:
  25.2 150.7 all-gather.1
where the time goes:
time: 275 us; the launch traced here: 271 us
  waiting for transfers between devices  130 us (47%)
  local copies, waits for them, and re-layouts  49.9 us (18%)
  matrix products  43.3 us (16%)
  other arithmetic  21.1 us (8%)
  between operations  14.2 us (5%)
  starting transfers between devices  13 us (5%)
    all_gather x1, waiting for transfers between devices, on_device(): piece = lax.all_gather(pairs, 'tile', axis=0, tiled=True)  124 us
    another operation x2, local copies, waits for them, and re-layouts  23.9 us
    dot_general x2, matrix products, partial_attend(): jnp.einsum('hqk,khd->qhd', probs.astype(jnp.bfloat16), heads_v, preferred...  18.3 us
    dot_general x2, matrix products, partial_attend(): jnp.einsum('qhd,khd->hqk', heads_q, heads_k, preferred_element_type=jnp.f...  17.1 us
    slice x1, local copies, waits for them, and re-layouts, update(): piece[:, :width]  15.1 us
    reduce_sum x2, other arithmetic, partial_attend(): total = jnp.sum(probs, axis=2)  14.9 us
    ppermute x1, starting transfers between devices, with_halo(): lax.ppermute(tail, axis, [(i, (i + 1) % count) for i in range(ends)])  5.73 us
  transfers between devices with their start and end apart: 4, of which 3 were waited for; matrix products, arithmetic and copies ran while one was open for 6% of the time, Pallas kernels for 0%

commit v1 on v0

v1 whole, which is shorter than its diff:
```python
import functools

import jax
import jax.numpy as jnp
from jax import lax
from jax.experimental import pallas as pl
from jax.experimental.pallas import tpu as pltpu
from jax.sharding import PartitionSpec as P

HEADS = 16
HEAD = 72
D = HEADS * HEAD
STRIP = 128
MARGIN = 64
TILES = 32
SLOTS = 8
GROUPS = 8
COLS = 3 * D // GROUPS
SPAN = 640
ROWS = 224
PAD = 80
Q_AT = 2 * HEAD
V_AT = HEAD - 8
CHUNK = 4
EXP_SCALE = 1.4426950408889634 / (HEAD ** 0.5)
MESH = pl.DeviceIdType.MESH
F32 = jnp.float32
BF16 = jnp.bfloat16
ORDER = (8, 9, 6, 10, 7, 11, 12, 4, 13, 5, 2, 14, 3, 15, 1)


def body(
    x_hbm, cond_ref, wm_hbm, wp_hbm, wo_hbm, marks,
    out_ref,
    x_ref, wm, wp, wo, mod_send, mod_recv, mod, proj, send, buf, keys, q4, near, whole, osend, mixed,
    ranks,
    load_sem, mod_ssem, mod_rsem, send_sem, recv_sem, fwd_ssem, fwd_rsem, wh_sem, o_ssem, o_rsem,
):
    me = lax.axis_index("tile")
    grp = lax.axis_index("grp")
    chip = me // 2
    core = me % 2
    sibling = me + 1 - 2 * core

    barrier = pltpu.get_barrier_semaphore()
    for off in range(1, GROUPS):
        pl.semaphore_signal(barrier, inc=1, device_id={"grp": (grp + off) % GROUPS}, device_id_type=MESH)
    for off in range(1, HEADS):
        pl.semaphore_signal(
            barrier, inc=1, device_id={"tile": ((chip + off) % HEADS) * 2 + core}, device_id_type=MESH
        )
    pl.semaphore_signal(barrier, inc=1, device_id={"tile": sibling}, device_id_type=MESH)

    load_m = pltpu.make_async_copy(wm_hbm, wm, load_sem.at[0])
    load_x = pltpu.make_async_copy(x_hbm, x_ref, load_sem.at[1])
    load_p = [
        pltpu.make_async_copy(wp_hbm.at[:, pl.ds(D * i, D)], wp.at[i], load_sem.at[2 + i]) for i in range(3)
    ]
    load_o = pltpu.make_async_copy(wo_hbm, wo, load_sem.at[5])
    load_m.start()
    load_x.start()
    for copy in load_p:
        copy.start()
    load_o.start()

    load_m.wait()
    mod_send[...] = jnp.zeros_like(mod_send)
    mod_send[:, :COLS] = jnp.dot(cond_ref[...], wm[...], preferred_element_type=F32)
    mod_send[...] = pltpu.roll(mod_send[...], (grp * COLS) % 128, axis=1)

    load_x.wait()
    values32 = x_ref[...].astype(F32)
    mean = jnp.mean(values32, axis=1, keepdims=True)
    centered = values32 - mean
    variance = jnp.mean(centered * centered, axis=1, keepdims=True)
    unit = centered / jnp.sqrt(variance + 1e-06)

    rank = jnp.int32(0)
    slots = [jnp.int32(0)] * (SLOTS // 2)
    for t in range(TILES):
        mark = marks[0, t]
        for j in range(SLOTS // 2):
            hit = jnp.logical_and(mark > 0, rank == core * (SLOTS // 2) + j)
            slots[j] = jnp.where(hit, jnp.int32(t), slots[j])
        ranks[t] = jnp.minimum(rank, SLOTS - 1)
        rank = rank + mark

    pl.semaphore_wait(barrier, GROUPS - 1 + HEADS - 1 + 1)

    mod_copies = []
    for off in range(1, GROUPS):
        copy = pltpu.make_async_remote_copy(
            src_ref=mod_send, dst_ref=mod_recv.at[off - 1],
            send_sem=mod_ssem.at[off - 1], recv_sem=mod_rsem.at[off - 1],
            device_id={"grp": (grp + off) % GROUPS}, device_id_type=MESH,
        )
        copy.start()
        mod_copies.append(copy)
    mod[...] = jnp.zeros_like(mod)

    def add_columns(source, block):
        base = pl.multiple_of((source * COLS) // 128 * 128, 128)
        mod[:, pl.ds(base, SPAN)] += block

    add_columns(grp, mod_send[...])
    for off in range(1, GROUPS):
        mod_copies[off - 1].wait_recv()
        add_columns((grp + GROUPS - off) % GROUPS, mod_recv[off - 1])
    row = mod[pl.ds(grp, 1), :]
    shift = row[:, :D]
    scale = row[:, D : 2 * D]
    gate = row[:, 2 * D : 3 * D]
    normed = (unit * (1.0 + scale) + shift).astype(BF16)

    for part in range(3):
        load_p[part].wait()
        block = jnp.dot(normed, wp[part], preferred_element_type=F32)
        proj[part] = block.T
    for h in range(HEADS):
        rows = pl.ds(h * HEAD, HEAD)
        send[h] = jnp.concatenate(
            [proj[1, rows, :], proj[2, rows, :], proj[0, rows, :], jnp.zeros((8, STRIP), F32)], axis=0
        ).astype(BF16)

    copies = []
    for off in ORDER:
        other = (chip + off) % HEADS
        copy = pltpu.make_async_remote_copy(
            src_ref=send.at[other], dst_ref=buf.at[me],
            send_sem=send_sem.at[off], recv_sem=recv_sem.at[off],
            device_id={"tile": other * 2 + core}, device_id_type=MESH,
        )
        copy.start()
        copies.append(copy)

    def forward(off, src):
        strip = ((chip + HEADS - off) % HEADS) * 2 + core
        return pltpu.make_async_remote_copy(
            src_ref=src, dst_ref=buf.at[strip],
            send_sem=fwd_ssem.at[off], recv_sem=fwd_rsem.at[off],
            device_id={"tile": sibling}, device_id_type=MESH,
        )

    def store_keys(strip):
        block = buf[strip, 0:PAD, :].astype(F32).T
        keys[pl.ds(pl.multiple_of((strip + 1) * STRIP, STRIP), STRIP), :] = block.astype(BF16)

    keys[pl.ds(0, STRIP), :] = jnp.zeros((STRIP, PAD), BF16)
    keys[pl.ds((TILES + 1) * STRIP, STRIP), :] = jnp.zeros((STRIP, PAD), BF16)
    forwards = [forward(0, send.at[chip])]
    forwards[0].start()
    buf[me] = send[chip]
    store_keys(me)
    for off, copy in zip(ORDER, copies):
        copy.wait_recv()
        strip = ((chip + HEADS - off) % HEADS) * 2 + core
        passed = forward(off, buf.at[strip])
        passed.start()
        forwards.append(passed)
        store_keys(strip)
    for off, passed in zip((0,) + ORDER, forwards):
        passed.wait_recv()
        store_keys(((chip + HEADS - off) % HEADS) * 2 + 1 - core)

    for j in range(SLOTS // 2):
        q4[:, j * STRIP : (j + 1) * STRIP] = buf[slots[j], Q_AT:ROWS, :]
    wide = (SLOTS // 2) * STRIP

    def whole_step(i, state):
        top, total, acc = state
        span = CHUNK * STRIP
        block = keys[pl.ds(pl.multiple_of(STRIP + i * span, STRIP), span), :]
        scores = jnp.dot(block, q4[...], preferred_element_type=F32)
        merged = jnp.maximum(top, jnp.max(scores, axis=0, keepdims=True))
        factor = jnp.exp2((top - merged) * EXP_SCALE)
        probs = jnp.exp2((scores - merged) * EXP_SCALE)
        total = total * factor + jnp.sum(probs, axis=0, keepdims=True)
        values = jnp.concatenate([buf[i * CHUNK + j, V_AT : V_AT + PAD, :] for j in range(CHUNK)], axis=1)
        acc = acc * factor + jnp.dot(values, probs.astype(BF16), preferred_element_type=F32)
        return merged, total, acc

    state = (
        jnp.full((1, wide), -1e30, F32), jnp.zeros((1, wide), F32), jnp.zeros((PAD, wide), F32),
    )
    _, total, acc = lax.fori_loop(0, TILES // CHUNK, whole_step, state)
    result = acc / total
    for j in range(SLOTS // 2):
        whole[core * (SLOTS // 2) + j] = result[8:PAD, j * STRIP : (j + 1) * STRIP]
    mine = whole.at[pl.ds(core * (SLOTS // 2), SLOTS // 2)]
    swap = pltpu.make_async_remote_copy(
        src_ref=mine, dst_ref=mine, send_sem=wh_sem.at[0], recv_sem=wh_sem.at[1],
        device_id={"tile": sibling}, device_id_type=MESH,
    )
    swap.start()

    def near_step(j, carry):
        strip = 2 * j + core
        block = keys[pl.ds(pl.multiple_of((strip + 1) * STRIP - MARGIN, MARGIN), 2 * STRIP), :]
        scores = jnp.dot(block, buf[strip, Q_AT:ROWS, :], preferred_element_type=F32)
        at = strip * STRIP - MARGIN + lax.broadcasted_iota(jnp.int32, scores.shape, 0)
        scores = jnp.where(jnp.logical_and(at >= 0, at < TILES * STRIP), scores, -1e30)
        probs = jnp.exp2((scores - jnp.max(scores, axis=0, keepdims=True)) * EXP_SCALE)
        sums = jnp.sum(probs, axis=0, keepdims=True)
        blank = jnp.zeros((MARGIN, STRIP), BF16)
        weights = jnp.concatenate([blank, probs.astype(BF16), blank], axis=0)
        rows = pl.ds(V_AT, PAD)
        values = jnp.concatenate(
            [
                buf[jnp.maximum(strip - 1, 0), rows, :],
                buf[strip, rows, :],
                buf[jnp.minimum(strip + 1, TILES - 1), rows, :],
            ],
            axis=1,
        )
        near[j] = (jnp.dot(values, weights, preferred_element_type=F32) / sums)[8:PAD]
        return carry

    lax.fori_loop(0, TILES // 2, near_step, 0, unroll=4)
    swap.wait_recv()

    for j in range(TILES // 2):
        strip = 2 * j + core
        extra = whole[ranks[strip]]
        total = near[j] + jnp.where(marks[0, strip] > 0, extra, 0.0)
        osend[j] = jnp.concatenate([total, jnp.zeros((PAD - HEAD, STRIP), F32)], axis=0).astype(BF16)
    outs = []
    for off in ORDER:
        other = (chip + off) % HEADS
        copy = pltpu.make_async_remote_copy(
            src_ref=osend.at[other], dst_ref=mixed.at[chip],
            send_sem=o_ssem.at[off], recv_sem=o_rsem.at[off],
            device_id={"tile": other * 2 + core}, device_id_type=MESH,
        )
        copy.start()
        outs.append(copy)
    mixed[chip] = osend[chip]
    load_o.wait()
    for copy in outs:
        copy.wait_recv()

    gathered = jnp.concatenate([mixed[h, 0:HEAD, :].astype(F32) for h in range(HEADS)], axis=0).T
    branch = jnp.dot(gathered.astype(BF16), wo[...], preferred_element_type=F32)
    out_ref[...] = (x_ref[...].astype(F32) + gate * branch).astype(BF16)

    for copy in mod_copies + copies + forwards + outs + [swap]:
        copy.wait_send()


def on_device(latents, condition, w_modulate, w_project, w_output, detail):
    hbm = pl.BlockSpec(memory_space=pl.ANY)
    vmem = pl.BlockSpec(memory_space=pltpu.VMEM)
    dma = pltpu.SemaphoreType.DMA
    updated = pl.pallas_call(
        body,
        out_shape=jax.ShapeDtypeStruct((STRIP, D), BF16),
        in_specs=[hbm, vmem, hbm, hbm, hbm, pl.BlockSpec(memory_space=pltpu.SMEM)],
        out_specs=vmem,
        scratch_shapes=[
            pltpu.VMEM((STRIP, D), BF16),
            pltpu.VMEM((D, COLS), BF16),
            pltpu.VMEM((3, D, D), BF16),
            pltpu.VMEM((D, D), BF16),
            pltpu.VMEM((GROUPS, SPAN), F32),
            pltpu.VMEM((GROUPS - 1, GROUPS, SPAN), F32),
            pltpu.VMEM((GROUPS, 3 * D + 256), F32),
            pltpu.VMEM((3, D, STRIP), F32),
            pltpu.VMEM((HEADS, ROWS, STRIP), BF16),
            pltpu.VMEM((TILES, ROWS, STRIP), BF16),
            pltpu.VMEM(((TILES + 2) * STRIP, PAD), BF16),
            pltpu.VMEM((PAD, SLOTS // 2 * STRIP), BF16),
            pltpu.VMEM((TILES // 2, HEAD, STRIP), F32),
            pltpu.VMEM((SLOTS, HEAD, STRIP), F32),
            pltpu.VMEM((HEADS, PAD, STRIP), BF16),
            pltpu.VMEM((HEADS, PAD, STRIP), BF16),
            pltpu.SMEM((TILES,), jnp.int32),
            dma((6,)),
            dma((GROUPS - 1,)), dma((GROUPS - 1,)),
            dma((HEADS,)), dma((HEADS,)),
            dma((HEADS,)), dma((HEADS,)),
            dma((2,)),
            dma((HEADS,)), dma((HEADS,)),
        ],
        compiler_params=pltpu.CompilerParams(
            collective_id=0, has_side_effects=True, vmem_limit_bytes=56 * 1024 * 1024
        ),
    )(latents[0], condition, w_modulate, w_project, w_output, detail)
    return updated[None]


def solution(mesh):
    in_specs = (P("grp", "tile", None), P(), P(None, "grp"), P(), P(), P("grp", None))
    out_specs = P("grp", "tile", None)
    return jax.shard_map(
        on_device, mesh=mesh, in_specs=in_specs, out_specs=out_specs, check_vma=False
    )
```

time: 275 us -> 67.9 us (0.25)
  the two profiles are of different devices: /device:TPU:99 before, /device:TPU:1 now
where the time goes in v1:
time: 67.9 us; the launch traced here: 67.8 us
  Pallas kernels  63.6 us (94%)
  local copies, waits for them, and re-layouts  4.12 us (6%)
    pallas_call x1, Pallas kernels, on_device(): pl.pallas_call(body, out_shape=jax.ShapeDtypeStruct((STRIP, D), BF16), in...  63.6 us
    unnamed x2, local copies, waits for them, and re-layouts  4.12 us

profile of v1, /device:TPU:1, one launch (start us, length us, event | category | flops | bytes accessed | tf_op | source)
XLA Modules:
  0.0 67.8 jit_solution(13068443499299581518)
XLA Ops:
  0.0 2.4 %copy.7.wm_hbm = bf16[1152,432]{1,0:T(8,128)(2,1)} copy(bf16[1152,432]{0,1:T(8,128)(2,1)} %param.8) | data formatting | bytes 1990656 | tf_op args[2]
  2.4 63.6 %shard_map.64 = bf16[128,1152]{1,0:T(8,128)(2,1)} custom-call(bf16[128,1152]{1,0:T(8,128)(2,1)} %bitcast.3, bf16[8,1152]{1,0:T(8,128)(2,1)} %cond_ref.1, bf16[1152,432]{1,0:T(8,128)(2,1)} %copy.7.wm_hbm, bf16[1152,3456]{1,0:T(8,128)(2,1)} %wp_hbm.1, bf16[1152,1152]{1,0:T(8,128)(2,1)} %wo_hbm.1, s32[1,32]{1,0:T(1,128)} %marks.1), custom_call_target="tpu_custom_call" | custom-call | tf_op jit(solution)/shard_map/pallas_call | solution.py:253
  66.1 1.7 %copy.9 = bf16[1,128,1152]{2,1,0:T(8,128)(2,1)} copy(bf16[1,128,1152]{2,1,0:T(8,128)(2,1)} %bitcast.2) | data formatting | bytes 589824

commit v2 on v1

v2 whole, which is shorter than its diff:
```python
import functools

import jax
import jax.numpy as jnp
from jax import lax
from jax.experimental import pallas as pl
from jax.experimental.pallas import tpu as pltpu
from jax.sharding import PartitionSpec as P

HEADS = 16
HEAD = 72
D = HEADS * HEAD
STRIP = 128
MARGIN = 64
TILES = 32
SLOTS = 8
GROUPS = 8
COLS = 3 * D // GROUPS
SPAN = 640
PAD = 80
V_AT = HEAD - 8
SIDE = SLOTS // 2
WIDE = SIDE * STRIP
TILE_ROWS = 5
EXP_SCALE = 1.4426950408889634 / (HEAD ** 0.5)
MESH = pl.DeviceIdType.MESH
F32 = jnp.float32
BF16 = jnp.bfloat16
ORDER = (8, 9, 6, 10, 7, 11, 12, 4, 13, 5, 2, 14, 3, 15, 1)


def body(
    x_hbm, cond_hbm, wm_hbm, wp_hbm, wo_hbm, marks_hbm,
    out_ref,
    x_ref, cond, wm, wp, wo, mod_cols, mod_send, mod_recv, mod, proj, qsend, kvsend, qbuf, kvbuf, keys, q4,
    near, whole, osend, mixed, marks, ranks,
    load_sem, mod_ssem, mod_rsem, q_ssem, q_rsem, kv_ssem, kv_rsem, qf_ssem, qf_rsem, kvf_ssem, kvf_rsem,
    wh_sem, o_ssem, o_rsem,
):
    me = lax.axis_index("tile")
    grp = lax.axis_index("grp")
    chip = me // 2
    core = me % 2
    sibling = me + 1 - 2 * core

    barrier = pltpu.get_barrier_semaphore()
    for off in ORDER:
        pl.semaphore_signal(
            barrier, inc=1, device_id={"tile": ((chip + off) % HEADS) * 2 + core}, device_id_type=MESH
        )
    for off in range(1, GROUPS):
        pl.semaphore_signal(barrier, inc=1, device_id={"grp": (grp + off) % GROUPS}, device_id_type=MESH)
    pl.semaphore_signal(barrier, inc=1, device_id={"tile": sibling}, device_id_type=MESH)

    load_c = pltpu.make_async_copy(cond_hbm, cond, load_sem.at[6])
    load_m = pltpu.make_async_copy(wm_hbm, wm, load_sem.at[0])
    load_x = pltpu.make_async_copy(x_hbm, x_ref, load_sem.at[1])
    load_d = pltpu.make_async_copy(marks_hbm, marks, load_sem.at[7])
    load_p = [
        pltpu.make_async_copy(wp_hbm.at[:, pl.ds(D * i, D)], wp.at[i], load_sem.at[2 + i]) for i in range(3)
    ]
    load_o = pltpu.make_async_copy(wo_hbm, wo, load_sem.at[5])
    for copy in [load_c, load_m, load_x, load_d] + load_p + [load_o]:
        copy.start()

    mod_cols[...] = jnp.zeros_like(mod_cols)
    mod_send[...] = jnp.zeros_like(mod_send)
    mod[...] = jnp.zeros_like(mod)
    load_c.wait()
    load_m.wait()
    mod_cols[:, :COLS] = lax.dot_general(
        cond[...], wm[...], (((1,), (1,)), ((), ())), preferred_element_type=F32
    )
    shifted = pltpu.roll(mod_cols[...], (grp * COLS) % 128, axis=1)
    for i in range(TILE_ROWS):
        mod_send[:, i, :] = shifted[:, i * 128 : (i + 1) * 128]

    load_x.wait()
    values32 = x_ref[...].astype(F32)
    mean = jnp.mean(values32, axis=1, keepdims=True)
    centered = values32 - mean
    variance = jnp.mean(centered * centered, axis=1, keepdims=True)
    unit = centered / jnp.sqrt(variance + 1e-06)

    load_d.wait()
    rank = jnp.int32(0)
    slots = [jnp.int32(0)] * SIDE
    for t in range(TILES):
        mark = marks[0, t]
        for j in range(SIDE):
            hit = jnp.logical_and(mark > 0, rank == core * SIDE + j)
            slots[j] = jnp.where(hit, jnp.int32(t), slots[j])
        ranks[t] = jnp.minimum(rank, SLOTS - 1)
        rank = rank + mark

    pl.semaphore_wait(barrier, GROUPS - 1 + HEADS - 1 + 1)

    mod_copies = []
    for off in range(1, GROUPS):
        image = (grp + off) % GROUPS
        copy = pltpu.make_async_remote_copy(
            src_ref=mod_send.at[image], dst_ref=mod_recv.at[off - 1],
            send_sem=mod_ssem.at[off - 1], recv_sem=mod_rsem.at[off - 1],
            device_id={"grp": image}, device_id_type=MESH,
        )
        copy.start()
        mod_copies.append(copy)

    def add_columns(source, block):
        rows = pl.ds((source * COLS) // 128, TILE_ROWS)
        mod[rows, :] += block[0:TILE_ROWS]

    add_columns(grp, mod_send[grp])
    for off in range(1, GROUPS):
        mod_copies[off - 1].wait_recv()
        add_columns((grp + GROUPS - off) % GROUPS, mod_recv[off - 1])

    def mod_row(part):
        first = part * D // 128
        return jnp.concatenate([mod[first + i : first + i + 1, :] for i in range(D // 128)], axis=1)

    normed = (unit * (1.0 + mod_row(1)) + mod_row(0)).astype(BF16)

    def project(part):
        load_p[part].wait()
        proj[part] = jnp.dot(normed, wp[part], preferred_element_type=F32).T

    def exchange(src, dst, ssem, rsem):
        sent = []
        for off in ORDER:
            other = (chip + off) % HEADS
            copy = pltpu.make_async_remote_copy(
                src_ref=src.at[other], dst_ref=dst, send_sem=ssem.at[off], recv_sem=rsem.at[off],
                device_id={"tile": other * 2 + core}, device_id_type=MESH,
            )
            copy.start()
            sent.append(copy)
        return sent

    def forward(off, src, dst, ssem, rsem):
        copy = pltpu.make_async_remote_copy(
            src_ref=src, dst_ref=dst.at[strip_of(off, core)], send_sem=ssem.at[off], recv_sem=rsem.at[off],
            device_id={"tile": sibling}, device_id_type=MESH,
        )
        copy.start()
        return copy

    def strip_of(off, parity):
        return ((chip + HEADS - off) % HEADS) * 2 + parity

    project(0)
    for h in range(HEADS):
        qsend[h] = jnp.concatenate(
            [proj[0, h * HEAD : (h + 1) * HEAD, :], jnp.zeros((PAD - HEAD, STRIP), F32)], axis=0
        ).astype(BF16)
    q_sent = exchange(qsend, qbuf.at[me], q_ssem, q_rsem)
    q_passed = [forward(0, qsend.at[chip], qbuf, qf_ssem, qf_rsem)]
    qbuf[me] = qsend[chip]
    project(1)
    project(2)
    for h in range(HEADS):
        rows = slice(h * HEAD, (h + 1) * HEAD)
        kvsend[h] = jnp.concatenate([proj[1, rows, :], proj[2, rows, :]], axis=0).astype(BF16)
    kv_sent = exchange(kvsend, kvbuf.at[me], kv_ssem, kv_rsem)
    kv_passed = [forward(0, kvsend.at[chip], kvbuf, kvf_ssem, kvf_rsem)]
    kvbuf[me] = kvsend[chip]
    keys[pl.ds(0, STRIP), :] = jnp.zeros((STRIP, PAD), BF16)
    keys[pl.ds((TILES + 1) * STRIP, STRIP), :] = jnp.zeros((STRIP, PAD), BF16)

    for off, copy in zip(ORDER, q_sent):
        copy.wait_recv()
        q_passed.append(forward(off, qbuf.at[strip_of(off, core)], qbuf, qf_ssem, qf_rsem))
    for copy in q_passed:
        copy.wait_recv()
    for j in range(SIDE):
        q4[:, j * STRIP : (j + 1) * STRIP] = qbuf[slots[j]]

    def whole_step(off, state):
        top, total, acc = state
        pair = (chip + HEADS - off) % HEADS
        for parity in range(2):
            strip = pair * 2 + parity
            block = kvbuf[strip, 0:PAD, :].astype(F32).T
            keys[pl.ds(pl.multiple_of((strip + 1) * STRIP, STRIP), STRIP), :] = block.astype(BF16)
        block = keys[pl.ds(pl.multiple_of((2 * pair + 1) * STRIP, STRIP), 2 * STRIP), :]
        scores = jnp.dot(block, q4[...], preferred_element_type=F32)
        merged = jnp.maximum(top, jnp.max(scores, axis=0, keepdims=True))
        factor = jnp.exp2((top - merged) * EXP_SCALE)
        probs = jnp.exp2((scores - merged) * EXP_SCALE)
        total = total * factor + jnp.sum(probs, axis=0, keepdims=True)
        rows = slice(V_AT, V_AT + PAD)
        values = jnp.concatenate([kvbuf[2 * pair, rows, :], kvbuf[2 * pair + 1, rows, :]], axis=1)
        acc = acc * factor + jnp.dot(values, probs.astype(BF16), preferred_element_type=F32)
        return merged, total, acc

    state = (
        jnp.full((1, WIDE), -1e30, F32), jnp.zeros((1, WIDE), F32), jnp.zeros((PAD, WIDE), F32),
    )
    steps = (0,) + ORDER
    for i, off in enumerate(steps):
        if i + 1 < len(steps):
            kv_sent[i].wait_recv()
            later = steps[i + 1]
            kv_passed.append(forward(later, kvbuf.at[strip_of(later, core)], kvbuf, kvf_ssem, kvf_rsem))
        kv_passed[i].wait_recv()
        state = whole_step(off, state)
    _, total, acc = state
    result = acc / total
    for j in range(SIDE):
        whole[core * SIDE + j] = result[8:PAD, j * STRIP : (j + 1) * STRIP]
    mine = whole.at[pl.ds(core * SIDE, SIDE)]
    swap = pltpu.make_async_remote_copy(
        src_ref=mine, dst_ref=mine, send_sem=wh_sem.at[0], recv_sem=wh_sem.at[1],
        device_id={"tile": sibling}, device_id_type=MESH,
    )
    swap.start()

    def near_step(j, carry):
        strip = 2 * j + core
        block = keys[pl.ds(pl.multiple_of((strip + 1) * STRIP - MARGIN, MARGIN), 2 * STRIP), :]
        scores = jnp.dot(block, qbuf[strip], preferred_element_type=F32)
        at = strip * STRIP - MARGIN + lax.broadcasted_iota(jnp.int32, scores.shape, 0)
        scores = jnp.where(jnp.logical_and(at >= 0, at < TILES * STRIP), scores, -1e30)
        probs = jnp.exp2((scores - jnp.max(scores, axis=0, keepdims=True)) * EXP_SCALE)
        sums = jnp.sum(probs, axis=0, keepdims=True)
        blank = jnp.zeros((MARGIN, STRIP), BF16)
        weights = jnp.concatenate([blank, probs.astype(BF16), blank], axis=0)
        rows = pl.ds(V_AT, PAD)
        values = jnp.concatenate(
            [
                kvbuf[jnp.maximum(strip - 1, 0), rows, :],
                kvbuf[strip, rows, :],
                kvbuf[jnp.minimum(strip + 1, TILES - 1), rows, :],
            ],
            axis=1,
        )
        near[j] = (jnp.dot(values, weights, preferred_element_type=F32) / sums)[8:PAD]
        return carry

    lax.fori_loop(0, TILES // 2, near_step, 0, unroll=4)
    swap.wait_recv()

    for j in range(TILES // 2):
        strip = 2 * j + core
        extra = whole[ranks[strip]]
        total = near[j] + jnp.where(marks[0, strip] > 0, extra, 0.0)
        osend[j] = jnp.concatenate(
            [total[8 * r : 8 * r + 8] for r in range(HEAD // 8)], axis=1
        ).astype(BF16)
    outs = exchange(osend, mixed.at[chip], o_ssem, o_rsem)
    mixed[chip] = osend[chip]
    load_o.wait()
    for copy in outs:
        copy.wait_recv()

    gathered = []
    for h in range(HEADS):
        block = mixed[h].astype(F32)
        gathered += [block[:, 128 * r : 128 * r + 128] for r in range(HEAD // 8)]
    gathered = jnp.concatenate(gathered, axis=0).T
    branch = jnp.dot(gathered.astype(BF16), wo[...], preferred_element_type=F32)
    out_ref[...] = (x_ref[...].astype(F32) + mod_row(2) * branch).astype(BF16)

    for copy in mod_copies + q_sent + q_passed + kv_sent + kv_passed + outs + [swap]:
        copy.wait_send()


def on_device(latents, condition, w_modulate, w_project, w_output, detail):
    hbm = pl.BlockSpec(memory_space=pl.ANY)
    dma = pltpu.SemaphoreType.DMA
    updated = pl.pallas_call(
        body,
        out_shape=jax.ShapeDtypeStruct((STRIP, D), BF16),
        in_specs=[hbm] * 6,
        out_specs=pl.BlockSpec(memory_space=pltpu.VMEM),
        scratch_shapes=[
            pltpu.VMEM((STRIP, D), BF16),
            pltpu.VMEM((GROUPS, D), BF16),
            pltpu.VMEM((COLS, D), BF16),
            pltpu.VMEM((3, D, D), BF16),
            pltpu.VMEM((D, D), BF16),
            pltpu.VMEM((GROUPS, SPAN), F32),
            pltpu.VMEM((GROUPS, 8, 128), F32),
            pltpu.VMEM((GROUPS - 1, 8, 128), F32),
            pltpu.VMEM((32, 128), F32),
            pltpu.VMEM((3, D, STRIP), F32),
            pltpu.VMEM((HEADS, PAD, STRIP), BF16),
            pltpu.VMEM((HEADS, 2 * HEAD, STRIP), BF16),
            pltpu.VMEM((TILES, PAD, STRIP), BF16),
            pltpu.VMEM((TILES, 2 * HEAD, STRIP), BF16),
            pltpu.VMEM(((TILES + 2) * STRIP, PAD), BF16),
            pltpu.VMEM((PAD, WIDE), BF16),
            pltpu.VMEM((TILES // 2, HEAD, STRIP), F32),
            pltpu.VMEM((SLOTS, HEAD, STRIP), F32),
            pltpu.VMEM((HEADS, 8, D), BF16),
            pltpu.VMEM((HEADS, 8, D), BF16),
            pltpu.SMEM((1, TILES), jnp.int32),
            pltpu.SMEM((TILES,), jnp.int32),
            dma((8,)),
            dma((GROUPS - 1,)), dma((GROUPS - 1,)),
            dma((HEADS,)), dma((HEADS,)),
            dma((HEADS,)), dma((HEADS,)),
            dma((HEADS,)), dma((HEADS,)),
            dma((HEADS,)), dma((HEADS,)),
            dma((2,)),
            dma((HEADS,)), dma((HEADS,)),
        ],
        compiler_params=pltpu.CompilerParams(
            collective_id=0, has_side_effects=True, vmem_limit_bytes=56 * 1024 * 1024
        ),
    )(latents[0], condition, w_modulate.T, w_project, w_output, detail)
    return updated[None]


def solution(mesh):
    in_specs = (P("grp", "tile", None), P(), P(None, "grp"), P(), P(), P("grp", None))
    out_specs = P("grp", "tile", None)
    return jax.shard_map(
        on_device, mesh=mesh, in_specs=in_specs, out_specs=out_specs, check_vma=False
    )
```

time: 67.9 us -> 63.2 us (0.931)
  local copies, waits for them, and re-layouts: 4.12 us -> 1.7 us
  Pallas kernels: 63.6 us -> 61.4 us
    unnamed x2 -> x1, local copies, waits for them, and re-layouts: 4.12 us -> 1.7 us
    pallas_call x1, Pallas kernels: 63.6 us -> 61.4 us  [on_device(): pl.pallas_call(body, out_shape=jax.ShapeDtypeStruct((STRIP, D), BF16), in...]
where the time goes in v2:
time: 63.2 us; the launch traced here: 63.1 us
  Pallas kernels  61.4 us (97%)
  local copies, waits for them, and re-layouts  1.7 us (3%)
    pallas_call x1, Pallas kernels, on_device(): pl.pallas_call(body, out_shape=jax.ShapeDtypeStruct((STRIP, D), BF16), in...  61.4 us
    unnamed x1, local copies, waits for them, and re-layouts  1.7 us

profile of v2, /device:TPU:1, one launch (start us, length us, event | category | flops | bytes accessed | tf_op | source)
XLA Modules:
  0.0 63.1 jit_solution(14457389023285682228)
XLA Ops:
  0.0 61.4 %shard_map.64 = bf16[128,1152]{1,0:T(8,128)(2,1)} custom-call(bf16[128,1152]{1,0:T(8,128)(2,1)} %bitcast.5, bf16[8,1152]{1,0:T(8,128)(2,1)} %cond_hbm.1, bf16[432,1152]{1,0:T(8,128)(2,1)} %bitcast.4, bf16[1152,3456]{1,0:T(8,128)(2,1)} %wp_hbm.1, bf16[1152,1152]{1,0:T(8,128)(2,1)} %wo_hbm.1, s32[1,32]{1,0:T(1,128)} %marks_hbm.1), custom_call_target="tpu_custom_call" | custom-call | tf_op jit(solution)/shard_map/pallas_call | solution.py:271
  61.4 1.7 %copy.8 = bf16[1,128,1152]{2,1,0:T(8,128)(2,1)} copy(bf16[1,128,1152]{2,1,0:T(8,128)(2,1)} %bitcast.3) | data formatting | bytes 589824

commit v3 on v2

--- a/solution.py
+++ b/solution.py
@@ -33,7 +33,7 @@
     x_hbm, cond_hbm, wm_hbm, wp_hbm, wo_hbm, marks_hbm,
     out_ref,
     x_ref, cond, wm, wp, wo, mod_cols, mod_send, mod_recv, mod, proj, qsend, kvsend, qbuf, kvbuf, keys, q4,
-    near, whole, osend, mixed, marks, ranks,
+    score_buf, near, whole, osend, mixed, marks, ranks,
     load_sem, mod_ssem, mod_rsem, q_ssem, q_rsem, kv_ssem, kv_rsem, qf_ssem, qf_rsem, kvf_ssem, kvf_rsem,
     wh_sem, o_ssem, o_rsem,
 ):
@@ -60,7 +60,7 @@
         pltpu.make_async_copy(wp_hbm.at[:, pl.ds(D * i, D)], wp.at[i], load_sem.at[2 + i]) for i in range(3)
     ]
     load_o = pltpu.make_async_copy(wo_hbm, wo, load_sem.at[5])
-    for copy in [load_c, load_m, load_x, load_d] + load_p + [load_o]:
+    for copy in (load_c, load_m, load_x, load_d):
         copy.start()
 
     mod_cols[...] = jnp.zeros_like(mod_cols)
@@ -68,12 +68,27 @@
     mod[...] = jnp.zeros_like(mod)
     load_c.wait()
     load_m.wait()
+    for copy in load_p + [load_o]:
+        copy.start()
     mod_cols[:, :COLS] = lax.dot_general(
         cond[...], wm[...], (((1,), (1,)), ((), ())), preferred_element_type=F32
     )
     shifted = pltpu.roll(mod_cols[...], (grp * COLS) % 128, axis=1)
     for i in range(TILE_ROWS):
         mod_send[:, i, :] = shifted[:, i * 128 : (i + 1) * 128]
+
+    pl.semaphore_wait(barrier, GROUPS - 1 + HEADS - 1 + 1)
+
+    mod_copies = []
+    for off in range(1, GROUPS):
+        image = (grp + off) % GROUPS
+        copy = pltpu.make_async_remote_copy(
+            src_ref=mod_send.at[image], dst_ref=mod_recv.at[off - 1],
+            send_sem=mod_ssem.at[off - 1], recv_sem=mod_rsem.at[off - 1],
+            device_id={"grp": image}, device_id_type=MESH,
+        )
+        copy.start()
+        mod_copies.append(copy)
 
     load_x.wait()
     values32 = x_ref[...].astype(F32)
@@ -93,19 +108,6 @@
         ranks[t] = jnp.minimum(rank, SLOTS - 1)
         rank = rank + mark
 
-    pl.semaphore_wait(barrier, GROUPS - 1 + HEADS - 1 + 1)
-
-    mod_copies = []
-    for off in range(1, GROUPS):
-        image = (grp + off) % GROUPS
-        copy = pltpu.make_async_remote_copy(
-            src_ref=mod_send.at[image], dst_ref=mod_recv.at[off - 1],
-            send_sem=mod_ssem.at[off - 1], recv_sem=mod_rsem.at[off - 1],
-            device_id={"grp": image}, device_id_type=MESH,
-        )
-        copy.start()
-        mod_copies.append(copy)
-
     def add_columns(source, block):
         rows = pl.ds((source * COLS) // 128, TILE_ROWS)
         mod[rows, :] += block[0:TILE_ROWS]
@@ -125,17 +127,14 @@
         load_p[part].wait()
         proj[part] = jnp.dot(normed, wp[part], preferred_element_type=F32).T
 
-    def exchange(src, dst, ssem, rsem):
-        sent = []
-        for off in ORDER:
-            other = (chip + off) % HEADS
-            copy = pltpu.make_async_remote_copy(
-                src_ref=src.at[other], dst_ref=dst, send_sem=ssem.at[off], recv_sem=rsem.at[off],
-                device_id={"tile": other * 2 + core}, device_id_type=MESH,
-            )
-            copy.start()
-            sent.append(copy)
-        return sent
+    def exchange(off, src, dst, ssem, rsem):
+        other = (chip + off) % HEADS
+        copy = pltpu.make_async_remote_copy(
+            src_ref=src.at[other], dst_ref=dst, send_sem=ssem.at[off], recv_sem=rsem.at[off],
+            device_id={"tile": other * 2 + core}, device_id_type=MESH,
+        )
+        copy.start()
+        return copy
 
     def forward(off, src, dst, ssem, rsem):
         copy = pltpu.make_async_remote_copy(
@@ -153,7 +152,7 @@
         qsend[h] = jnp.concatenate(
             [proj[0, h * HEAD : (h + 1) * HEAD, :], jnp.zeros((PAD - HEAD, STRIP), F32)], axis=0
         ).astype(BF16)
-    q_sent = exchange(qsend, qbuf.at[me], q_ssem, q_rsem)
+    q_sent = [exchange(off, qsend, qbuf.at[me], q_ssem, q_rsem) for off in ORDER]
     q_passed = [forward(0, qsend.at[chip], qbuf, qf_ssem, qf_rsem)]
     qbuf[me] = qsend[chip]
     project(1)
@@ -161,12 +160,15 @@
     for h in range(HEADS):
         rows = slice(h * HEAD, (h + 1) * HEAD)
         kvsend[h] = jnp.concatenate([proj[1, rows, :], proj[2, rows, :]], axis=0).astype(BF16)
-    kv_sent = exchange(kvsend, kvbuf.at[me], kv_ssem, kv_rsem)
+    kv_sent = []
     kv_passed = [forward(0, kvsend.at[chip], kvbuf, kvf_ssem, kvf_rsem)]
     kvbuf[me] = kvsend[chip]
     keys[pl.ds(0, STRIP), :] = jnp.zeros((STRIP, PAD), BF16)
     keys[pl.ds((TILES + 1) * STRIP, STRIP), :] = jnp.zeros((STRIP, PAD), BF16)
 
+    for off, copy in zip(ORDER, q_sent):
+        copy.wait_send()
+        kv_sent.append(exchange(off, kvsend, kvbuf.at[me], kv_ssem, kv_rsem))
     for off, copy in zip(ORDER, q_sent):
         copy.wait_recv()
         q_passed.append(forward(off, qbuf.at[strip_of(off, core)], qbuf, qf_ssem, qf_rsem))
@@ -175,48 +177,33 @@
     for j in range(SIDE):
         q4[:, j * STRIP : (j + 1) * STRIP] = qbuf[slots[j]]
 
-    def whole_step(off, state):
-        top, total, acc = state
-        pair = (chip + HEADS - off) % HEADS
+    def pair_of(off):
+        return (chip + HEADS - off) % HEADS
+
+    def scores_step(i, off, top):
+        pair = pair_of(off)
         for parity in range(2):
             strip = pair * 2 + parity
             block = kvbuf[strip, 0:PAD, :].astype(F32).T
             keys[pl.ds(pl.multiple_of((strip + 1) * STRIP, STRIP), STRIP), :] = block.astype(BF16)
         block = keys[pl.ds(pl.multiple_of((2 * pair + 1) * STRIP, STRIP), 2 * STRIP), :]
         scores = jnp.dot(block, q4[...], preferred_element_type=F32)
-        merged = jnp.maximum(top, jnp.max(scores, axis=0, keepdims=True))
-        factor = jnp.exp2((top - merged) * EXP_SCALE)
-        probs = jnp.exp2((scores - merged) * EXP_SCALE)
+        score_buf[i % 2] = scores
+        return jnp.maximum(top, jnp.max(scores, axis=0, keepdims=True))
+
+    def values_step(i, off, before, top, total, acc):
+        pair = pair_of(off)
+        factor = jnp.exp2((before - top) * EXP_SCALE)
+        probs = jnp.exp2((score_buf[i % 2] - top) * EXP_SCALE)
         total = total * factor + jnp.sum(probs, axis=0, keepdims=True)
         rows = slice(V_AT, V_AT + PAD)
         values = jnp.concatenate([kvbuf[2 * pair, rows, :], kvbuf[2 * pair + 1, rows, :]], axis=1)
         acc = acc * factor + jnp.dot(values, probs.astype(BF16), preferred_element_type=F32)
-        return merged, total, acc
-
-    state = (
-        jnp.full((1, WIDE), -1e30, F32), jnp.zeros((1, WIDE), F32), jnp.zeros((PAD, WIDE), F32),
-    )
-    steps = (0,) + ORDER
-    for i, off in enumerate(steps):
-        if i + 1 < len(steps):
-            kv_sent[i].wait_recv()
-            later = steps[i + 1]
-            kv_passed.append(forward(later, kvbuf.at[strip_of(later, core)], kvbuf, kvf_ssem, kvf_rsem))
-        kv_passed[i].wait_recv()
-        state = whole_step(off, state)
-    _, total, acc = state
-    result = acc / total
-    for j in range(SIDE):
-        whole[core * SIDE + j] = result[8:PAD, j * STRIP : (j + 1) * STRIP]
-    mine = whole.at[pl.ds(core * SIDE, SIDE)]
-    swap = pltpu.make_async_remote_copy(
-        src_ref=mine, dst_ref=mine, send_sem=wh_sem.at[0], recv_sem=wh_sem.at[1],
-        device_id={"tile": sibling}, device_id_type=MESH,
-    )
-    swap.start()
-
-    def near_step(j, carry):
-        strip = 2 * j + core
+        return total, acc
+
+    def near_step(off):
+        pair = pair_of(off)
+        strip = 2 * pair + core
         block = keys[pl.ds(pl.multiple_of((strip + 1) * STRIP - MARGIN, MARGIN), 2 * STRIP), :]
         scores = jnp.dot(block, qbuf[strip], preferred_element_type=F32)
         at = strip * STRIP - MARGIN + lax.broadcasted_iota(jnp.int32, scores.shape, 0)
@@ -234,10 +221,43 @@
             ],
             axis=1,
         )
-        near[j] = (jnp.dot(values, weights, preferred_element_type=F32) / sums)[8:PAD]
-        return carry
-
-    lax.fori_loop(0, TILES // 2, near_step, 0, unroll=4)
+        near[pair] = (jnp.dot(values, weights, preferred_element_type=F32) / sums)[8:PAD]
+
+    steps = (0,) + ORDER
+    total = jnp.zeros((1, WIDE), F32)
+    acc = jnp.zeros((PAD, WIDE), F32)
+    tops = [jnp.full((1, WIDE), -1e30, F32)]
+    ready = []
+    done = 0
+    for i, off in enumerate(steps):
+        if i + 1 < len(steps):
+            kv_sent[i].wait_recv()
+            later = steps[i + 1]
+            kv_passed.append(forward(later, kvbuf.at[strip_of(later, core)], kvbuf, kvf_ssem, kvf_rsem))
+        kv_passed[i].wait_recv()
+        tops.append(scores_step(i, off, tops[i]))
+        if i > 0:
+            total, acc = values_step(i - 1, steps[i - 1], tops[i - 1], tops[i], total, acc)
+            for strip_off in ready[done:]:
+                near_step(strip_off)
+            done = len(ready)
+        come = steps[: i + 1]
+        for o in come:
+            if o not in ready and (o + 1) % HEADS in come and (o - 1) % HEADS in come:
+                ready.append(o)
+    last = len(steps) - 1
+    total, acc = values_step(last, steps[last], tops[last], tops[last + 1], total, acc)
+    result = acc / total
+    for j in range(SIDE):
+        whole[core * SIDE + j] = result[8:PAD, j * STRIP : (j + 1) * STRIP]
+    mine = whole.at[pl.ds(core * SIDE, SIDE)]
+    swap = pltpu.make_async_remote_copy(
+        src_ref=mine, dst_ref=mine, send_sem=wh_sem.at[0], recv_sem=wh_sem.at[1],
+        device_id={"tile": sibling}, device_id_type=MESH,
+    )
+    swap.start()
+    for strip_off in ready[done:]:
+        near_step(strip_off)
     swap.wait_recv()
 
     for j in range(TILES // 2):
@@ -247,7 +267,7 @@
         osend[j] = jnp.concatenate(
             [total[8 * r : 8 * r + 8] for r in range(HEAD // 8)], axis=1
         ).astype(BF16)
-    outs = exchange(osend, mixed.at[chip], o_ssem, o_rsem)
+    outs = [exchange(off, osend, mixed.at[chip], o_ssem, o_rsem) for off in ORDER]
     mixed[chip] = osend[chip]
     load_o.wait()
     for copy in outs:
@@ -261,7 +281,7 @@
     branch = jnp.dot(gathered.astype(BF16), wo[...], preferred_element_type=F32)
     out_ref[...] = (x_ref[...].astype(F32) + mod_row(2) * branch).astype(BF16)
 
-    for copy in mod_copies + q_sent + q_passed + kv_sent + kv_passed + outs + [swap]:
+    for copy in mod_copies + q_passed + kv_sent + kv_passed + outs + [swap]:
         copy.wait_send()
 
 
@@ -290,6 +310,7 @@
             pltpu.VMEM((TILES, 2 * HEAD, STRIP), BF16),
             pltpu.VMEM(((TILES + 2) * STRIP, PAD), BF16),
             pltpu.VMEM((PAD, WIDE), BF16),
+            pltpu.VMEM((2, 2 * STRIP, WIDE), F32),
             pltpu.VMEM((TILES // 2, HEAD, STRIP), F32),
             pltpu.VMEM((SLOTS, HEAD, STRIP), F32),
             pltpu.VMEM((HEADS, 8, D), BF16),

time: 63.2 us -> 60.8 us (0.962)
  Pallas kernels: 61.4 us -> 58.9 us
    pallas_call x1, Pallas kernels: 61.4 us -> 58.9 us  [on_device(): pl.pallas_call(body, out_shape=jax.ShapeDtypeStruct((STRIP, D), BF16), in...]
where the time goes in v3:
time: 60.8 us; the launch traced here: 60.6 us
  Pallas kernels  58.9 us (97%)
  local copies, waits for them, and re-layouts  1.7 us (3%)
    pallas_call x1, Pallas kernels, on_device(): pl.pallas_call(body, out_shape=jax.ShapeDtypeStruct((STRIP, D), BF16), in...  58.9 us
    unnamed x1, local copies, waits for them, and re-layouts  1.7 us

profile of v3, /device:TPU:1, one launch (start us, length us, event | category | flops | bytes accessed | tf_op | source)
XLA Modules:
  0.0 60.6 jit_solution(17176782395965701489)
XLA Ops:
  0.0 58.9 %shard_map.64 = bf16[128,1152]{1,0:T(8,128)(2,1)} custom-call(bf16[128,1152]{1,0:T(8,128)(2,1)} %bitcast.5, bf16[8,1152]{1,0:T(8,128)(2,1)} %cond_hbm.1, bf16[432,1152]{1,0:T(8,128)(2,1)} %bitcast.4, bf16[1152,3456]{1,0:T(8,128)(2,1)} %wp_hbm.1, bf16[1152,1152]{1,0:T(8,128)(2,1)} %wo_hbm.1, s32[1,32]{1,0:T(1,128)} %marks_hbm.1), custom_call_target="tpu_custom_call" | custom-call | tf_op jit(solution)/shard_map/pallas_call | solution.py:291
  58.9 1.7 %copy.8 = bf16[1,128,1152]{2,1,0:T(8,128)(2,1)} copy(bf16[1,128,1152]{2,1,0:T(8,128)(2,1)} %bitcast.3) | data formatting | bytes 589824

commit v4 on v3

--- a/solution.py
+++ b/solution.py
@@ -22,6 +22,7 @@
 SIDE = SLOTS // 2
 WIDE = SIDE * STRIP
 TILE_ROWS = 5
+AHEAD = 2
 EXP_SCALE = 1.4426950408889634 / (HEAD ** 0.5)
 MESH = pl.DeviceIdType.MESH
 F32 = jnp.float32
@@ -230,17 +231,18 @@
     ready = []
     done = 0
     for i, off in enumerate(steps):
-        if i + 1 < len(steps):
-            kv_sent[i].wait_recv()
-            later = steps[i + 1]
+        while len(kv_passed) < min(i + AHEAD + 1, len(steps)):
+            kv_sent[len(kv_passed) - 1].wait_recv()
+            later = steps[len(kv_passed)]
             kv_passed.append(forward(later, kvbuf.at[strip_of(later, core)], kvbuf, kvf_ssem, kvf_rsem))
         kv_passed[i].wait_recv()
         tops.append(scores_step(i, off, tops[i]))
         if i > 0:
             total, acc = values_step(i - 1, steps[i - 1], tops[i - 1], tops[i], total, acc)
-            for strip_off in ready[done:]:
-                near_step(strip_off)
-            done = len(ready)
+            if i + 1 < len(steps):
+                for strip_off in ready[done:]:
+                    near_step(strip_off)
+                done = len(ready)
         come = steps[: i + 1]
         for o in come:
             if o not in ready and (o + 1) % HEADS in come and (o - 1) % HEADS in come:
@@ -290,7 +292,7 @@
     dma = pltpu.SemaphoreType.DMA
     updated = pl.pallas_call(
         body,
-        out_shape=jax.ShapeDtypeStruct((STRIP, D), BF16),
+        out_shape=pltpu.VMEM((STRIP, D), BF16),
         in_specs=[hbm] * 6,
         out_specs=pl.BlockSpec(memory_space=pltpu.VMEM),
         scratch_shapes=[

time: 60.8 us -> 57.4 us (0.944)
  Pallas kernels: 58.9 us -> 56.6 us
  local copies, waits for them, and re-layouts: 1.7 us -> 0.72 us
    pallas_call x1, Pallas kernels: 58.9 us -> 56.6 us  [on_device(): pl.pallas_call(body, out_shape=pltpu.VMEM((STRIP, D), BF16), in_specs=[hb...]
    unnamed x1, local copies, waits for them, and re-layouts: 1.7 us -> 0.72 us
where the time goes in v4:
time: 57.4 us; the launch traced here: 57.3 us
  Pallas kernels  56.6 us (99%)
  local copies, waits for them, and re-layouts  0.72 us (1%)
    pallas_call x1, Pallas kernels, on_device(): pl.pallas_call(body, out_shape=pltpu.VMEM((STRIP, D), BF16), in_specs=[hb...  56.6 us

profile of v4, /device:TPU:1, one launch (start us, length us, event | category | flops | bytes accessed | tf_op | source)
XLA Modules:
  0.0 57.3 jit_solution(9787448747878598909)
XLA Ops:
  0.0 56.6 %shard_map.64 = bf16[128,1152]{1,0:T(8,128)(2,1)S(1)} custom-call(bf16[128,1152]{1,0:T(8,128)(2,1)} %bitcast.5, bf16[8,1152]{1,0:T(8,128)(2,1)} %cond_hbm.1, bf16[432,1152]{1,0:T(8,128)(2,1)} %bitcast.4, bf16[1152,3456]{1,0:T(8,128)(2,1)} %wp_hbm.1, bf16[1152,1152]{1,0:T(8,128)(2,1)} %wo_hbm.1, s32[1,32]{1,0:T(1,128)} %marks_hbm.1), custom_call_target="tpu_custom_call" | custom-call | tf_op jit(solution)/shard_map/pallas_call | solution.py:293
  56.6 0.7 %copy.8 = bf16[1,128,1152]{2,1,0:T(8,128)(2,1)} copy(bf16[1,128,1152]{2,1,0:T(8,128)(2,1)S(1)} %bitcast.3) | data formatting | bytes 589824

commit v5 on v4

--- a/solution.py
+++ b/solution.py
@@ -27,14 +27,28 @@
 MESH = pl.DeviceIdType.MESH
 F32 = jnp.float32
 BF16 = jnp.bfloat16
-ORDER = (8, 9, 6, 10, 7, 11, 12, 4, 13, 5, 2, 14, 3, 15, 1)
+ORDER = (1, 15, 3, 14, 2, 5, 13, 4, 12, 11, 7, 10, 6, 9, 8)
+PARTS = (0, 128, 256, COLS)
+
+
+def side_by_side(block):
+    return jnp.concatenate([block[8 * r : 8 * r + 8] for r in range(HEAD // 8)], axis=1).astype(BF16)
+
+
+def stacked(message):
+    block = message.astype(F32)
+    return [block[:, 128 * r : 128 * r + 128] for r in range(HEAD // 8)]
+
+
+def queries(message):
+    return jnp.concatenate(stacked(message) + [jnp.zeros((PAD - HEAD, STRIP), F32)], axis=0).astype(BF16)
 
 
 def body(
     x_hbm, cond_hbm, wm_hbm, wp_hbm, wo_hbm, marks_hbm,
     out_ref,
     x_ref, cond, wm, wp, wo, mod_cols, mod_send, mod_recv, mod, proj, qsend, kvsend, qbuf, kvbuf, keys, q4,
-    score_buf, near, whole, osend, mixed, marks, ranks,
+    score_buf, near, whole, branch, osend, mixed, marks, ranks,
     load_sem, mod_ssem, mod_rsem, q_ssem, q_rsem, kv_ssem, kv_rsem, qf_ssem, qf_rsem, kvf_ssem, kvf_rsem,
     wh_sem, o_ssem, o_rsem,
 ):
@@ -54,21 +68,25 @@
     pl.semaphore_signal(barrier, inc=1, device_id={"tile": sibling}, device_id_type=MESH)
 
     load_c = pltpu.make_async_copy(cond_hbm, cond, load_sem.at[6])
-    load_m = pltpu.make_async_copy(wm_hbm, wm, load_sem.at[0])
+    load_m = [
+        pltpu.make_async_copy(wm_hbm.at[pl.ds(a, b - a)], wm.at[pl.ds(a, b - a)], load_sem.at[8 + i])
+        for i, (a, b) in enumerate(zip(PARTS, PARTS[1:]))
+    ]
     load_x = pltpu.make_async_copy(x_hbm, x_ref, load_sem.at[1])
     load_d = pltpu.make_async_copy(marks_hbm, marks, load_sem.at[7])
     load_p = [
         pltpu.make_async_copy(wp_hbm.at[:, pl.ds(D * i, D)], wp.at[i], load_sem.at[2 + i]) for i in range(3)
     ]
     load_o = pltpu.make_async_copy(wo_hbm, wo, load_sem.at[5])
-    for copy in (load_c, load_m, load_x, load_d):
+    for copy in [load_c] + load_m + [load_x, load_d]:
         copy.start()
 
     mod_cols[...] = jnp.zeros_like(mod_cols)
     mod_send[...] = jnp.zeros_like(mod_send)
     mod[...] = jnp.zeros_like(mod)
     load_c.wait()
-    load_m.wait()
+    for copy in load_m:
+        copy.wait()
     for copy in load_p + [load_o]:
         copy.start()
     mod_cols[:, :COLS] = lax.dot_general(
@@ -150,9 +168,7 @@
 
     project(0)
     for h in range(HEADS):
-        qsend[h] = jnp.concatenate(
-            [proj[0, h * HEAD : (h + 1) * HEAD, :], jnp.zeros((PAD - HEAD, STRIP), F32)], axis=0
-        ).astype(BF16)
+        qsend[h] = side_by_side(proj[0, h * HEAD : (h + 1) * HEAD, :])
     q_sent = [exchange(off, qsend, qbuf.at[me], q_ssem, q_rsem) for off in ORDER]
     q_passed = [forward(0, qsend.at[chip], qbuf, qf_ssem, qf_rsem)]
     qbuf[me] = qsend[chip]
@@ -176,7 +192,7 @@
     for copy in q_passed:
         copy.wait_recv()
     for j in range(SIDE):
-        q4[:, j * STRIP : (j + 1) * STRIP] = qbuf[slots[j]]
+        q4[:, j * STRIP : (j + 1) * STRIP] = queries(qbuf[slots[j]])
 
     def pair_of(off):
         return (chip + HEADS - off) % HEADS
@@ -206,7 +222,7 @@
         pair = pair_of(off)
         strip = 2 * pair + core
         block = keys[pl.ds(pl.multiple_of((strip + 1) * STRIP - MARGIN, MARGIN), 2 * STRIP), :]
-        scores = jnp.dot(block, qbuf[strip], preferred_element_type=F32)
+        scores = jnp.dot(block, queries(qbuf[strip]), preferred_element_type=F32)
         at = strip * STRIP - MARGIN + lax.broadcasted_iota(jnp.int32, scores.shape, 0)
         scores = jnp.where(jnp.logical_and(at >= 0, at < TILES * STRIP), scores, -1e30)
         probs = jnp.exp2((scores - jnp.max(scores, axis=0, keepdims=True)) * EXP_SCALE)
@@ -266,22 +282,22 @@
         strip = 2 * j + core
         extra = whole[ranks[strip]]
         total = near[j] + jnp.where(marks[0, strip] > 0, extra, 0.0)
-        osend[j] = jnp.concatenate(
-            [total[8 * r : 8 * r + 8] for r in range(HEAD // 8)], axis=1
-        ).astype(BF16)
+        osend[j] = side_by_side(total)
     outs = [exchange(off, osend, mixed.at[chip], o_ssem, o_rsem) for off in ORDER]
     mixed[chip] = osend[chip]
     load_o.wait()
-    for copy in outs:
+
+    def project_head(head):
+        block = jnp.concatenate(stacked(mixed[head]), axis=0).T
+        return jnp.dot(block.astype(BF16), wo[head], preferred_element_type=F32)
+
+    branch[...] = project_head(chip)
+    for off, copy in zip(ORDER, outs):
         copy.wait_recv()
-
-    gathered = []
-    for h in range(HEADS):
-        block = mixed[h].astype(F32)
-        gathered += [block[:, 128 * r : 128 * r + 128] for r in range(HEAD // 8)]
-    gathered = jnp.concatenate(gathered, axis=0).T
-    branch = jnp.dot(gathered.astype(BF16), wo[...], preferred_element_type=F32)
-    out_ref[...] = (x_ref[...].astype(F32) + mod_row(2) * branch).astype(BF16)
+        if off != ORDER[-1]:
+            branch[...] += project_head((chip + HEADS - off) % HEADS)
+    result = branch[...] + project_head((chip + HEADS - ORDER[-1]) % HEADS)
+    out_ref[...] = (x_ref[...].astype(F32) + mod_row(2) * result).astype(BF16)
 
     for copy in mod_copies + q_passed + kv_sent + kv_passed + outs + [swap]:
         copy.wait_send()
@@ -300,26 +316,27 @@
             pltpu.VMEM((GROUPS, D), BF16),
             pltpu.VMEM((COLS, D), BF16),
             pltpu.VMEM((3, D, D), BF16),
-            pltpu.VMEM((D, D), BF16),
+            pltpu.VMEM((HEADS, HEAD, D), BF16),
             pltpu.VMEM((GROUPS, SPAN), F32),
             pltpu.VMEM((GROUPS, 8, 128), F32),
             pltpu.VMEM((GROUPS - 1, 8, 128), F32),
             pltpu.VMEM((32, 128), F32),
             pltpu.VMEM((3, D, STRIP), F32),
-            pltpu.VMEM((HEADS, PAD, STRIP), BF16),
+            pltpu.VMEM((HEADS, 8, D), BF16),
             pltpu.VMEM((HEADS, 2 * HEAD, STRIP), BF16),
-            pltpu.VMEM((TILES, PAD, STRIP), BF16),
+            pltpu.VMEM((TILES, 8, D), BF16),
             pltpu.VMEM((TILES, 2 * HEAD, STRIP), BF16),
             pltpu.VMEM(((TILES + 2) * STRIP, PAD), BF16),
             pltpu.VMEM((PAD, WIDE), BF16),
             pltpu.VMEM((2, 2 * STRIP, WIDE), F32),
             pltpu.VMEM((TILES // 2, HEAD, STRIP), F32),
             pltpu.VMEM((SLOTS, HEAD, STRIP), F32),
+            pltpu.VMEM((STRIP, D), F32),
             pltpu.VMEM((HEADS, 8, D), BF16),
             pltpu.VMEM((HEADS, 8, D), BF16),
             pltpu.SMEM((1, TILES), jnp.int32),
             pltpu.SMEM((TILES,), jnp.int32),
-            dma((8,)),
+            dma((11,)),
             dma((GROUPS - 1,)), dma((GROUPS - 1,)),
             dma((HEADS,)), dma((HEADS,)),
             dma((HEADS,)), dma((HEADS,)),
@@ -331,7 +348,7 @@
         compiler_params=pltpu.CompilerParams(
             collective_id=0, has_side_effects=True, vmem_limit_bytes=56 * 1024 * 1024
         ),
-    )(latents[0], condition, w_modulate.T, w_project, w_output, detail)
+    )(latents[0], condition, w_modulate.T, w_project, w_output.reshape(HEADS, HEAD, D), detail)
     return updated[None]
 
 

time: 57.4 us -> 54.9 us (0.956)
  Pallas kernels: 56.6 us -> 53.6 us
    pallas_call x1, Pallas kernels: 56.6 us -> 53.6 us  [on_device(): pl.pallas_call(body, out_shape=pltpu.VMEM((STRIP, D), BF16), in_specs=[hb...]
where the time goes in v5:
time: 54.9 us; the launch traced here: 54.4 us
  Pallas kernels  53.6 us (98%)
  local copies, waits for them, and re-layouts  0.72 us (1%)
    pallas_call x1, Pallas kernels, on_device(): pl.pallas_call(body, out_shape=pltpu.VMEM((STRIP, D), BF16), in_specs=[hb...  53.6 us

profile of v5, /device:TPU:1, one launch (start us, length us, event | category | flops | bytes accessed | tf_op | source)
XLA Modules:
  0.0 54.4 jit_solution(7768871527479189526)
XLA Ops:
  0.0 53.6 %shard_map.64 = bf16[128,1152]{1,0:T(8,128)(2,1)S(1)} custom-call(bf16[128,1152]{1,0:T(8,128)(2,1)} %bitcast.7, bf16[8,1152]{1,0:T(8,128)(2,1)} %cond_hbm.1, bf16[432,1152]{1,0:T(8,128)(2,1)} %bitcast.6, bf16[1152,3456]{1,0:T(8,128)(2,1)} %wp_hbm.1, bf16[16,72,1152]{2,1,0:T(8,128)(2,1)} %bitcast.5, s32[1,32]{1,0:T(1,128)} %marks_hbm.1), custom_call_target="tpu_custom_call" | custom-call | tf_op jit(solution)/shard_map/pallas_call | solution.py:309
  53.6 0.7 %copy.8 = bf16[1,128,1152]{2,1,0:T(8,128)(2,1)} copy(bf16[1,128,1152]{2,1,0:T(8,128)(2,1)S(1)} %bitcast.4) | data formatting | bytes 589824

commit v6 on v5

--- a/solution.py
+++ b/solution.py
@@ -23,6 +23,7 @@
 WIDE = SIDE * STRIP
 TILE_ROWS = 5
 AHEAD = 2
+EARLY = 9
 EXP_SCALE = 1.4426950408889634 / (HEAD ** 0.5)
 MESH = pl.DeviceIdType.MESH
 F32 = jnp.float32
@@ -50,7 +51,7 @@
     x_ref, cond, wm, wp, wo, mod_cols, mod_send, mod_recv, mod, proj, qsend, kvsend, qbuf, kvbuf, keys, q4,
     score_buf, near, whole, branch, osend, mixed, marks, ranks,
     load_sem, mod_ssem, mod_rsem, q_ssem, q_rsem, kv_ssem, kv_rsem, qf_ssem, qf_rsem, kvf_ssem, kvf_rsem,
-    wh_sem, o_ssem, o_rsem,
+    wh_sem, o_ssem, o_rsem, rounds,
 ):
     me = lax.axis_index("tile")
     grp = lax.axis_index("grp")
@@ -59,13 +60,18 @@
     sibling = me + 1 - 2 * core
 
     barrier = pltpu.get_barrier_semaphore()
-    for off in ORDER:
-        pl.semaphore_signal(
-            barrier, inc=1, device_id={"tile": ((chip + off) % HEADS) * 2 + core}, device_id_type=MESH
-        )
+    around = [(me + 4) % TILES, (me + TILES - 4) % TILES]
+    for near_by in around + [me + 2 - 4 * (chip % 2), sibling]:
+        pl.semaphore_signal(barrier, inc=1, device_id={"tile": near_by}, device_id_type=MESH)
     for off in range(1, GROUPS):
         pl.semaphore_signal(barrier, inc=1, device_id={"grp": (grp + off) % GROUPS}, device_id_type=MESH)
-    pl.semaphore_signal(barrier, inc=1, device_id={"tile": sibling}, device_id_type=MESH)
+
+    def tell(step):
+        for near_by in around:
+            pl.semaphore_signal(rounds.at[step], inc=1, device_id={"tile": near_by}, device_id_type=MESH)
+
+    def hear(step):
+        pl.semaphore_wait(rounds.at[step], 2)
 
     load_c = pltpu.make_async_copy(cond_hbm, cond, load_sem.at[6])
     load_m = [
@@ -96,7 +102,7 @@
     for i in range(TILE_ROWS):
         mod_send[:, i, :] = shifted[:, i * 128 : (i + 1) * 128]
 
-    pl.semaphore_wait(barrier, GROUPS - 1 + HEADS - 1 + 1)
+    pl.semaphore_wait(barrier, GROUPS - 1 + 4)
 
     mod_copies = []
     for off in range(1, GROUPS):
@@ -109,12 +115,16 @@
         copy.start()
         mod_copies.append(copy)
 
+    tell(0)
     load_x.wait()
     values32 = x_ref[...].astype(F32)
     mean = jnp.mean(values32, axis=1, keepdims=True)
     centered = values32 - mean
     variance = jnp.mean(centered * centered, axis=1, keepdims=True)
     unit = centered / jnp.sqrt(variance + 1e-06)
+
+    hear(0)
+    tell(1)
 
     load_d.wait()
     rank = jnp.int32(0)
@@ -127,11 +137,16 @@
         ranks[t] = jnp.minimum(rank, SLOTS - 1)
         rank = rank + mark
 
+    hear(1)
+    tell(2)
+
     def add_columns(source, block):
         rows = pl.ds((source * COLS) // 128, TILE_ROWS)
         mod[rows, :] += block[0:TILE_ROWS]
 
     add_columns(grp, mod_send[grp])
+    hear(2)
+    tell(3)
     for off in range(1, GROUPS):
         mod_copies[off - 1].wait_recv()
         add_columns((grp + GROUPS - off) % GROUPS, mod_recv[off - 1])
@@ -169,6 +184,7 @@
     project(0)
     for h in range(HEADS):
         qsend[h] = side_by_side(proj[0, h * HEAD : (h + 1) * HEAD, :])
+    hear(3)
     q_sent = [exchange(off, qsend, qbuf.at[me], q_ssem, q_rsem) for off in ORDER]
     q_passed = [forward(0, qsend.at[chip], qbuf, qf_ssem, qf_rsem)]
     qbuf[me] = qsend[chip]
@@ -287,16 +303,20 @@
     mixed[chip] = osend[chip]
     load_o.wait()
 
-    def project_head(head):
-        block = jnp.concatenate(stacked(mixed[head]), axis=0).T
-        return jnp.dot(block.astype(BF16), wo[head], preferred_element_type=F32)
-
-    branch[...] = project_head(chip)
-    for off, copy in zip(ORDER, outs):
+    def project_heads(heads):
+        total = None
+        for head in heads:
+            block = jnp.concatenate(stacked(mixed[head]), axis=0).T
+            part = jnp.dot(block.astype(BF16), wo[head], preferred_element_type=F32)
+            total = part if total is None else total + part
+        return total
+
+    for copy in outs[:EARLY]:
         copy.wait_recv()
-        if off != ORDER[-1]:
-            branch[...] += project_head((chip + HEADS - off) % HEADS)
-    result = branch[...] + project_head((chip + HEADS - ORDER[-1]) % HEADS)
+    branch[...] = project_heads([chip] + [pair_of(off) for off in ORDER[:EARLY]])
+    for copy in outs[EARLY:]:
+        copy.wait_recv()
+    result = branch[...] + project_heads([pair_of(off) for off in ORDER[EARLY:]])
     out_ref[...] = (x_ref[...].astype(F32) + mod_row(2) * result).astype(BF16)
 
     for copy in mod_copies + q_passed + kv_sent + kv_passed + outs + [swap]:
@@ -344,6 +364,7 @@
             dma((HEADS,)), dma((HEADS,)),
             dma((2,)),
             dma((HEADS,)), dma((HEADS,)),
+            pltpu.SemaphoreType.REGULAR((4,)),
         ],
         compiler_params=pltpu.CompilerParams(
             collective_id=0, has_side_effects=True, vmem_limit_bytes=56 * 1024 * 1024

time: 54.9 us -> 55.8 us (1.016)
  Pallas kernels: 53.6 us -> 55 us
    pallas_call x1, Pallas kernels: 53.6 us -> 55 us  [on_device(): pl.pallas_call(body, out_shape=pltpu.VMEM((STRIP, D), BF16), in_specs=[hb...]
where the time goes in v6:
time: 55.8 us; the launch traced here: 55.7 us
  Pallas kernels  55 us (99%)
  local copies, waits for them, and re-layouts  0.72 us (1%)
    pallas_call x1, Pallas kernels, on_device(): pl.pallas_call(body, out_shape=pltpu.VMEM((STRIP, D), BF16), in_specs=[hb...  55 us

profile of v6, /device:TPU:1, one launch (start us, length us, event | category | flops | bytes accessed | tf_op | source)
XLA Modules:
  0.0 55.7 jit_solution(12431601151629967228)
XLA Ops:
  0.0 55.0 %shard_map.64 = bf16[128,1152]{1,0:T(8,128)(2,1)S(1)} custom-call(bf16[128,1152]{1,0:T(8,128)(2,1)} %bitcast.7, bf16[8,1152]{1,0:T(8,128)(2,1)} %cond_hbm.1, bf16[432,1152]{1,0:T(8,128)(2,1)} %bitcast.6, bf16[1152,3456]{1,0:T(8,128)(2,1)} %wp_hbm.1, bf16[16,72,1152]{2,1,0:T(8,128)(2,1)} %bitcast.5, s32[1,32]{1,0:T(1,128)} %marks_hbm.1), custom_call_target="tpu_custom_call" | custom-call | tf_op jit(solution)/shard_map/pallas_call | solution.py:329
  55.0 0.7 %copy.8 = bf16[1,128,1152]{2,1,0:T(8,128)(2,1)} copy(bf16[1,128,1152]{2,1,0:T(8,128)(2,1)S(1)} %bitcast.4) | data formatting | bytes 589824

commit v7 on v6

--- a/solution.py
+++ b/solution.py
@@ -60,14 +60,16 @@
     sibling = me + 1 - 2 * core
 
     barrier = pltpu.get_barrier_semaphore()
-    around = [(me + 4) % TILES, (me + TILES - 4) % TILES]
-    for near_by in around + [me + 2 - 4 * (chip % 2), sibling]:
+    across = me + 2 - 4 * (chip % 2)
+    around = [[(me + far) % TILES, (me + TILES - far) % TILES] for far in (8, 4)]
+    near_peers = around[0] + around[1] + [across, (across + 4) % TILES, (across + TILES - 4) % TILES, sibling]
+    for near_by in near_peers:
         pl.semaphore_signal(barrier, inc=1, device_id={"tile": near_by}, device_id_type=MESH)
     for off in range(1, GROUPS):
         pl.semaphore_signal(barrier, inc=1, device_id={"grp": (grp + off) % GROUPS}, device_id_type=MESH)
 
     def tell(step):
-        for near_by in around:
+        for near_by in around[step]:
             pl.semaphore_signal(rounds.at[step], inc=1, device_id={"tile": near_by}, device_id_type=MESH)
 
     def hear(step):
@@ -102,7 +104,7 @@
     for i in range(TILE_ROWS):
         mod_send[:, i, :] = shifted[:, i * 128 : (i + 1) * 128]
 
-    pl.semaphore_wait(barrier, GROUPS - 1 + 4)
+    pl.semaphore_wait(barrier, GROUPS - 1 + len(near_peers))
 
     mod_copies = []
     for off in range(1, GROUPS):
@@ -137,16 +139,11 @@
         ranks[t] = jnp.minimum(rank, SLOTS - 1)
         rank = rank + mark
 
-    hear(1)
-    tell(2)
-
     def add_columns(source, block):
         rows = pl.ds((source * COLS) // 128, TILE_ROWS)
         mod[rows, :] += block[0:TILE_ROWS]
 
     add_columns(grp, mod_send[grp])
-    hear(2)
-    tell(3)
     for off in range(1, GROUPS):
         mod_copies[off - 1].wait_recv()
         add_columns((grp + GROUPS - off) % GROUPS, mod_recv[off - 1])
@@ -184,7 +181,7 @@
     project(0)
     for h in range(HEADS):
         qsend[h] = side_by_side(proj[0, h * HEAD : (h + 1) * HEAD, :])
-    hear(3)
+    hear(1)
     q_sent = [exchange(off, qsend, qbuf.at[me], q_ssem, q_rsem) for off in ORDER]
     q_passed = [forward(0, qsend.at[chip], qbuf, qf_ssem, qf_rsem)]
     qbuf[me] = qsend[chip]
@@ -364,7 +361,7 @@
             dma((HEADS,)), dma((HEADS,)),
             dma((2,)),
             dma((HEADS,)), dma((HEADS,)),
-            pltpu.SemaphoreType.REGULAR((4,)),
+            pltpu.SemaphoreType.REGULAR((2,)),
         ],
         compiler_params=pltpu.CompilerParams(
             collective_id=0, has_side_effects=True, vmem_limit_bytes=56 * 1024 * 1024

time: 55.8 us -> 54.3 us (0.973)
  Pallas kernels: 55 us -> 53.4 us
    pallas_call x1, Pallas kernels: 55 us -> 53.4 us  [on_device(): pl.pallas_call(body, out_shape=pltpu.VMEM((STRIP, D), BF16), in_specs=[hb...]
where the time goes in v7:
time: 54.3 us; the launch traced here: 54.2 us
  Pallas kernels  53.4 us (98%)
  local copies, waits for them, and re-layouts  0.72 us (1%)
    pallas_call x1, Pallas kernels, on_device(): pl.pallas_call(body, out_shape=pltpu.VMEM((STRIP, D), BF16), in_specs=[hb...  53.4 us

profile of v7, /device:TPU:1, one launch (start us, length us, event | category | flops | bytes accessed | tf_op | source)
XLA Modules:
  0.0 54.2 jit_solution(42748322246722736)
XLA Ops:
  0.0 53.4 %shard_map.64 = bf16[128,1152]{1,0:T(8,128)(2,1)S(1)} custom-call(bf16[128,1152]{1,0:T(8,128)(2,1)} %bitcast.7, bf16[8,1152]{1,0:T(8,128)(2,1)} %cond_hbm.1, bf16[432,1152]{1,0:T(8,128)(2,1)} %bitcast.6, bf16[1152,3456]{1,0:T(8,128)(2,1)} %wp_hbm.1, bf16[16,72,1152]{2,1,0:T(8,128)(2,1)} %bitcast.5, s32[1,32]{1,0:T(1,128)} %marks_hbm.1), custom_call_target="tpu_custom_call" | custom-call | tf_op jit(solution)/shard_map/pallas_call | solution.py:326
  53.4 0.7 %copy.8 = bf16[1,128,1152]{2,1,0:T(8,128)(2,1)} copy(bf16[1,128,1152]{2,1,0:T(8,128)(2,1)S(1)} %bitcast.4) | data formatting | bytes 589824

commit v8 on v7

--- a/solution.py
+++ b/solution.py
@@ -23,7 +23,6 @@
 WIDE = SIDE * STRIP
 TILE_ROWS = 5
 AHEAD = 2
-EARLY = 9
 EXP_SCALE = 1.4426950408889634 / (HEAD ** 0.5)
 MESH = pl.DeviceIdType.MESH
 F32 = jnp.float32
@@ -49,7 +48,7 @@
     x_hbm, cond_hbm, wm_hbm, wp_hbm, wo_hbm, marks_hbm,
     out_ref,
     x_ref, cond, wm, wp, wo, mod_cols, mod_send, mod_recv, mod, proj, qsend, kvsend, qbuf, kvbuf, keys, q4,
-    score_buf, near, whole, branch, osend, mixed, marks, ranks,
+    score_buf, near, whole, osend, mixed, marks, ranks,
     load_sem, mod_ssem, mod_rsem, q_ssem, q_rsem, kv_ssem, kv_rsem, qf_ssem, qf_rsem, kvf_ssem, kvf_rsem,
     wh_sem, o_ssem, o_rsem, rounds,
 ):
@@ -296,24 +295,14 @@
         extra = whole[ranks[strip]]
         total = near[j] + jnp.where(marks[0, strip] > 0, extra, 0.0)
         osend[j] = side_by_side(total)
-    outs = [exchange(off, osend, mixed.at[chip], o_ssem, o_rsem) for off in ORDER]
+    outs = [exchange(off, osend, mixed.at[chip], o_ssem, o_rsem) for off in reversed(ORDER)]
     mixed[chip] = osend[chip]
     load_o.wait()
 
-    def project_heads(heads):
-        total = None
-        for head in heads:
-            block = jnp.concatenate(stacked(mixed[head]), axis=0).T
-            part = jnp.dot(block.astype(BF16), wo[head], preferred_element_type=F32)
-            total = part if total is None else total + part
-        return total
-
-    for copy in outs[:EARLY]:
+    for copy in outs:
         copy.wait_recv()
-    branch[...] = project_heads([chip] + [pair_of(off) for off in ORDER[:EARLY]])
-    for copy in outs[EARLY:]:
-        copy.wait_recv()
-    result = branch[...] + project_heads([pair_of(off) for off in ORDER[EARLY:]])
+    gathered = jnp.concatenate([row for h in range(HEADS) for row in stacked(mixed[h])], axis=0).T
+    result = jnp.dot(gathered.astype(BF16), wo[...], preferred_element_type=F32)
     out_ref[...] = (x_ref[...].astype(F32) + mod_row(2) * result).astype(BF16)
 
     for copy in mod_copies + q_passed + kv_sent + kv_passed + outs + [swap]:
@@ -333,7 +322,7 @@
             pltpu.VMEM((GROUPS, D), BF16),
             pltpu.VMEM((COLS, D), BF16),
             pltpu.VMEM((3, D, D), BF16),
-            pltpu.VMEM((HEADS, HEAD, D), BF16),
+            pltpu.VMEM((D, D), BF16),
             pltpu.VMEM((GROUPS, SPAN), F32),
             pltpu.VMEM((GROUPS, 8, 128), F32),
             pltpu.VMEM((GROUPS - 1, 8, 128), F32),
@@ -348,7 +337,6 @@
             pltpu.VMEM((2, 2 * STRIP, WIDE), F32),
             pltpu.VMEM((TILES // 2, HEAD, STRIP), F32),
             pltpu.VMEM((SLOTS, HEAD, STRIP), F32),
-            pltpu.VMEM((STRIP, D), F32),
             pltpu.VMEM((HEADS, 8, D), BF16),
             pltpu.VMEM((HEADS, 8, D), BF16),
             pltpu.SMEM((1, TILES), jnp.int32),
@@ -366,7 +354,7 @@
         compiler_params=pltpu.CompilerParams(
             collective_id=0, has_side_effects=True, vmem_limit_bytes=56 * 1024 * 1024
         ),
-    )(latents[0], condition, w_modulate.T, w_project, w_output.reshape(HEADS, HEAD, D), detail)
+    )(latents[0], condition, w_modulate.T, w_project, w_output, detail)
     return updated[None]
 
 

time: 54.3 us -> 53.4 us (0.983)
  Pallas kernels: 53.4 us -> 52.6 us
    pallas_call x1, Pallas kernels: 53.4 us -> 52.6 us  [on_device(): pl.pallas_call(body, out_shape=pltpu.VMEM((STRIP, D), BF16), in_specs=[hb...]
where the time goes in v8:
time: 53.4 us; the launch traced here: 53.3 us
  Pallas kernels  52.6 us (99%)
  local copies, waits for them, and re-layouts  0.72 us (1%)
    pallas_call x1, Pallas kernels, on_device(): pl.pallas_call(body, out_shape=pltpu.VMEM((STRIP, D), BF16), in_specs=[hb...  52.6 us

profile of v8, /device:TPU:1, one launch (start us, length us, event | category | flops | bytes accessed | tf_op | source)
XLA Modules:
  0.0 53.3 jit_solution(7200559715435623777)
XLA Ops:
  0.0 52.6 %shard_map.64 = bf16[128,1152]{1,0:T(8,128)(2,1)S(1)} custom-call(bf16[128,1152]{1,0:T(8,128)(2,1)} %bitcast.5, bf16[8,1152]{1,0:T(8,128)(2,1)} %cond_hbm.1, bf16[432,1152]{1,0:T(8,128)(2,1)} %bitcast.4, bf16[1152,3456]{1,0:T(8,128)(2,1)} %wp_hbm.1, bf16[1152,1152]{1,0:T(8,128)(2,1)} %wo_hbm.1, s32[1,32]{1,0:T(1,128)} %marks_hbm.1), custom_call_target="tpu_custom_call" | custom-call | tf_op jit(solution)/shard_map/pallas_call | solution.py:315
  52.6 0.7 %copy.8 = bf16[1,128,1152]{2,1,0:T(8,128)(2,1)} copy(bf16[1,128,1152]{2,1,0:T(8,128)(2,1)S(1)} %bitcast.3) | data formatting | bytes 589824
